TPU v7x, 32 devices: a whole 2x2x4 slice. The times are simulated.
32 devices in a mesh: dp: 4 (over z), expert: 8 (over y, x, core).
Axes of the slice: x: 2, y: 2, z: 4, core: 2. Of those that a mesh axis runs over, the one named last changes fastest.
Arguments:
- tokens: bfloat16 [256, 192, 1024], P(None, ('dp', 'expert')), may hold values from -200 to 200
- grad_out: bfloat16 [256, 192, 1024], P(None, ('dp', 'expert')), may hold values from -6 to 6
- slot_out: bfloat16 [512, 192, 1024], P('expert', 'dp'), may hold values from -6 to 6
- slot_params: bfloat16 [512, 1024], P('expert'), may hold values from -2 to 2
Outputs:
- grad_tokens: bfloat16 [256, 192, 1024], P(None, ('dp', 'expert'))
- grad_slot_out: bfloat16 [512, 192, 1024], P('expert', 'dp')
- grad_params: float32 [512, 1024], P('expert', 'dp')
All inputs are finite; a program needn't handle non-finite values.
Results may differ from a plain program's by a relative error of at most 0.018.
Values may be sent and summed in bfloat16 or wider, within the bound.
A program may use at most 128 MiB of HBM per device.

v0:
```python
import jax
import jax.numpy as jnp
from jax import lax
from jax.sharding import PartitionSpec as P


def fetch_outputs(slot_out, owners):
    own_slots, img_all, width = slot_out.shape
    shaped = slot_out.reshape(own_slots, owners, img_all // owners, width)
    arrived = lax.all_to_all(shaped, "expert", split_axis=1, concat_axis=0, tiled=True)
    return arrived.reshape(own_slots * owners, img_all // owners, width)


def return_grads(grad_slot, owners):
    all_slots, img_rows, width = grad_slot.shape
    shaped = grad_slot.reshape(owners, all_slots // owners, img_rows, width)
    arrived = lax.all_to_all(shaped, "expert", split_axis=0, concat_axis=2, tiled=True)
    return arrived.reshape(all_slots // owners, owners * img_rows, width)


def logit_grads(grad_comb, combine):
    rowdot = jnp.sum(combine * grad_comb, axis=-1, keepdims=True)
    return (combine * (grad_comb - rowdot)).astype(jnp.bfloat16)


def per_device(tokens, grad_out, slot_out, slot_params):
    owners = lax.axis_size("expert")
    all_params = lax.all_gather(slot_params, "expert", axis=0, tiled=True)
    logits = jnp.einsum("tbd,sd->tbs", tokens, all_params, preferred_element_type=jnp.float32)
    combine = jax.nn.softmax(logits, axis=-1)
    combine_low = combine.astype(jnp.bfloat16)
    slot_rows = fetch_outputs(slot_out, owners)
    grad_slot = jnp.einsum(
        "tbs,tbd->sbd", combine_low, grad_out, preferred_element_type=jnp.float32
    ).astype(jnp.bfloat16)
    grad_slot_out = return_grads(grad_slot, owners)
    grad_comb = jnp.einsum("tbd,sbd->tbs", grad_out, slot_rows, preferred_element_type=jnp.float32)
    grad_logits = logit_grads(grad_comb, combine)
    grad_tok = jnp.einsum(
        "tbs,sd->tbd", grad_logits, all_params, preferred_element_type=jnp.float32
    ).astype(jnp.bfloat16)
    param_part = jnp.einsum("tbs,tbd->sd", grad_logits, tokens, preferred_element_type=jnp.float32)
    owned = lax.psum_scatter(
        param_part.astype(jnp.bfloat16), "expert", scatter_dimension=0, tiled=True
    )
    grad_params = lax.psum_scatter(owned, "dp", scatter_dimension=1, tiled=True).astype(jnp.float32)
    return (grad_tok, grad_slot_out, grad_params)


def solution(mesh):
    return jax.shard_map(
        per_device,
        mesh=mesh,
        in_specs=(
            P(None, ("dp", "expert"), None),
            P(None, ("dp", "expert"), None),
            P("expert", "dp", None),
            P("expert", None),
        ),
        out_specs=(P(None, ("dp", "expert"), None), P("expert", "dp", None), P("expert", "dp")),
        check_vma=False,
    )
```

profile of v0, /device:TPU:0, one launch (start us, length us, event | category | flops | bytes accessed | tf_op | source)
XLA Modules:
  0.0 202.6 jit_solution(12654161094282766128)
XLA Ops:
  7.2 0.0 copy-start
  7.2 9.1 %copy.12 = bf16[64,48,1024]{2,0,1:T(8,128)(2,1)} copy(bf16[64,48,1024]{2,1,0:T(8,128)(2,1)} %param.6) | data formatting | bytes 12582912 | tf_op args[2]
  16.3 5.2 %all-to-all-start = ((bf16[64,8,6,1024]{3,0,2,1:T(8,128)(2,1)}), bf16[64,8,6,1024]{3,0,2,1:T(8,128)(2,1)}, u32[]{:S(2)}, u32[]{:S(2)}) async-start(bf16[64,8,6,1024]{3,0,2,1:T(8,128)(2,1)} %bitcast.38), calls=%async_computation | async-start | bytes 12582912 | tf_op jit(solution)/shard_map/all_to_all | solution.py:10
  21.5 0.0 all-gather.2.cloned.1.call-start
  21.6 0.7 all-gather.2.cloned.1.call-update
  22.3 45.9 %all-gather.2.cloned.1.call-done = bf16[512,1024]{1,0:T(8,128)(2,1)} async-done(((bf16[64,1024]{1,0:T(8,128)(2,1)}), bf16[512,1024]{1,0:T(8,128)(2,1)}) %all-gather.2.cloned.1.call-update) | async-done | bytes 1048592 | tf_op jit(solution)/shard_map/all_gather | solution.py:28
  68.2 4.1 %fusion.6 = f32[256,6,512]{2,0,1:T(8,128)S(1)} fusion(bf16[256,6,1024]{2,0,1:T(8,128)(2,1)} %param.4, bf16[512,1024]{1,0:T(8,128)(2,1)} %all-gather.2.cloned.1.call-done), kind=kOutput, calls=%fused_computation.13 | convolution fusion | flops 1610612736 | bytes 7340032 | tf_op jit(solution)/shard_map/tbd,sd->tbs/dot_general | solution.py:29
  72.3 0.0 copy-start.2
  72.3 2.5 %fusion.8 = (f32[256,6]{0,1:T(8,128)S(1)}, f32[256,6,512]{2,0,1:T(8,128)}) fusion(f32[256,6,512]{2,0,1:T(8,128)S(1)} %fusion.6), kind=kOutput, calls=%fused_computation.15 | output fusion | flops 1573375 | bytes 6297600 | tf_op jit(solution)/shard_map/sub | solution.py:30
  74.8 0.1 copy-done.2
  74.9 0.0 copy-done
  74.9 11.4 %convolution_convert_fusion = bf16[6,512,1024]{2,1,0:T(8,128)(2,1)} fusion(bf16[256,6,1024]{2,0,1:T(8,128)(2,1)S(1)} %copy-done, f32[256,6]{0,1:T(8,128)S(1)} %get-tuple-element.6, f32[256,6,512]{2,0,1:T(8,128)} %copy-done.2), kind=kOutput, calls=%fused_computation.1 | convolution fusion | flops 1616119808 | bytes 12589056 | tf_op jit(solution)/shard_map/tbs,tbd->sbd/dot_general | solution.py:33
  86.3 6.7 %copy.16 = bf16[8,64,6,1024]{3,1,2,0:T(8,128)(2,1)} copy(bf16[8,64,6,1024]{3,1,0,2:T(8,128)(2,1)} %bitcast.40) | data formatting | bytes 12582912 | tf_op jit(solution)/shard_map/reshape | solution.py:16
  93.0 4.6 %all-to-all-done = bf16[64,8,6,1024]{3,0,2,1:T(8,128)(2,1)} async-done(((bf16[64,8,6,1024]{3,0,2,1:T(8,128)(2,1)}), bf16[64,8,6,1024]{3,0,2,1:T(8,128)(2,1)}, u32[]{:S(2)}, u32[]{:S(2)}) %all-to-all-start) | async-done | bytes 6291488 | tf_op jit(solution)/shard_map/all_to_all | solution.py:10
  97.6 4.8 %all-to-all-start.1 = ((bf16[8,64,6,1024]{3,1,2,0:T(8,128)(2,1)}), bf16[8,64,6,1024]{3,1,2,0:T(8,128)(2,1)}, u32[]{:S(2)}, u32[]{:S(2)}) async-start(bf16[8,64,6,1024]{3,1,2,0:T(8,128)(2,1)} %copy.16), calls=%async_computation.1 | async-start | bytes 12582912 | tf_op jit(solution)/shard_map/all_to_all | solution.py:17
  102.4 0.2 reduce-scatter.3.cloned.1.call-start
  102.6 0.0 copy-start.1
  102.7 3.7 %copy.13 = bf16[8,64,1,6,1024]{4,1,0,3,2:T(8,128)(2,1)S(1)} copy(bf16[8,64,1,6,1024]{4,1,3,0,2:T(8,128)(2,1)} %bitcast.3) | data formatting | bytes 12582912 | tf_op jit(solution)/shard_map/all_to_all | solution.py:10
  106.3 0.0 copy-done.1
  106.4 2.0 fusion.1
  108.3 0.0 copy-start.4
  108.3 0.6 fusion.3
  109.0 0.0 copy-start.3
  109.0 1.1 copy-done.3
  110.1 0.7 copy-done.4
  110.8 2.8 %bitcast_convert_fusion = bf16[512,1024]{1,0:T(8,128)(2,1)} fusion(bf16[256,6,512]{2,0,1:T(8,128)(2,1)S(1)} %fusion.3, bf16[256,6,1024]{2,0,1:T(8,128)(2,1)S(1)} %copy-done.4), kind=kOutput, calls=%fused_computation.9 | convolution fusion | flops 1611137024 | bytes 5767168 | tf_op jit(solution)/shard_map/tbs,tbd->sd/dot_general | solution.py:42
  113.6 0.0 reduce-scatter.3.cloned.1.call-update
  113.6 0.0 reduce-scatter.5.cloned.1.call-start
  113.7 60.1 %reduce-scatter.3.cloned.1.call-done = bf16[64,1024]{1,0:T(8,128)(2,1)} async-done(((bf16[512,1024]{1,0:T(8,128)(2,1)}), bf16[64,1024]{1,0:T(8,128)(2,1)}) %reduce-scatter.3.cloned.1.call-update) | async-done | bytes 131088 | tf_op jit(solution)/shard_map/reduce_scatter | solution.py:43
  173.8 0.0 reduce-scatter.5.cloned.1.call-update
  173.8 5.2 %convolution_convert_fusion.1 = bf16[256,6,1024]{2,0,1:T(8,128)(2,1)} fusion(bf16[256,6,512]{2,0,1:T(8,128)(2,1)} %copy-done.3, bf16[512,1024]{1,0:T(8,128)(2,1)} %all-gather.2.cloned.1.call-done), kind=kOutput, calls=%fused_computation.8 | convolution fusion | flops 1612185600 | bytes 5767168 | tf_op jit(solution)/shard_map/tbs,sd->tbd/dot_general | solution.py:39
  179.0 0.0 all-to-all-done.1
  179.0 9.0 %copy.18 = bf16[64,48,1024]{2,1,0:T(8,128)(2,1)} copy(bf16[64,48,1024]{2,0,1:T(8,128)(2,1)} %bitcast.10) | data formatting | bytes 12582912
  188.0 6.6 %reduce-scatter.5.cloned.1.call-done = bf16[64,256]{1,0:T(8,128)(2,1)} async-done(((bf16[64,1024]{1,0:T(8,128)(2,1)}), bf16[64,256]{1,0:T(8,128)(2,1)}) %reduce-scatter.5.cloned.1.call-update) | async-done | bytes 32784 | tf_op jit(solution)/shard_map/reduce_scatter | solution.py:46
  194.6 1.4 convert_element_type.27
Async XLA Ops:
  7.2 67.7 %copy-start = (bf16[256,6,1024]{2,0,1:T(8,128)(2,1)S(1)}, bf16[256,6,1024]{2,0,1:T(8,128)(2,1)}, u32[]{:S(2)}) copy-start(bf16[256,6,1024]{2,0,1:T(8,128)(2,1)} %param.5) | copy-start | bytes 9437188
  16.3 81.3 %all-to-all-start = ((bf16[64,8,6,1024]{3,0,2,1:T(8,128)(2,1)}), bf16[64,8,6,1024]{3,0,2,1:T(8,128)(2,1)}, u32[]{:S(2)}, u32[]{:S(2)}) async-start(bf16[64,8,6,1024]{3,0,2,1:T(8,128)(2,1)} %bitcast.38), calls=%async_computation | async-start | bytes 12582912 | tf_op jit(solution)/shard_map/all_to_all | solution.py:10
  21.5 46.6 %all-gather.2.cloned.1.call-start = ((), (), s32[]{:S(2)}) async-start(), calls=%async_computation.4 | async-start | bytes 1179648 | tf_op jit(solution)/shard_map/all_gather | solution.py:28
  72.3 2.7 %copy-start.2 = (f32[256,6,512]{2,0,1:T(8,128)}, f32[256,6,512]{2,0,1:T(8,128)S(1)}, u32[]{:S(2)}) copy-start(f32[256,6,512]{2,0,1:T(8,128)S(1)} %fusion.6) | copy-start | bytes 9437188
  97.6 81.4 %all-to-all-start.1 = ((bf16[8,64,6,1024]{3,1,2,0:T(8,128)(2,1)}), bf16[8,64,6,1024]{3,1,2,0:T(8,128)(2,1)}, u32[]{:S(2)}, u32[]{:S(2)}) async-start(bf16[8,64,6,1024]{3,1,2,0:T(8,128)(2,1)} %copy.16), calls=%async_computation.1 | async-start | bytes 12582912 | tf_op jit(solution)/shard_map/all_to_all | solution.py:17
  102.4 71.4 %reduce-scatter.3.cloned.1.call-start = ((), (), s32[]{:S(2)}) async-start(), calls=%async_computation.5 | async-start | bytes 1179648 | tf_op jit(solution)/shard_map/reduce_scatter | solution.py:43
  102.6 3.7 %copy-start.1 = (f32[256,6,512]{2,0,1:T(8,128)S(1)}, f32[256,6,512]{2,0,1:T(8,128)}, u32[]{:S(2)}) copy-start(f32[256,6,512]{2,0,1:T(8,128)} %get-tuple-element.7) | copy-start | bytes 9437188
  108.3 2.5 %copy-start.4 = (bf16[256,6,1024]{2,0,1:T(8,128)(2,1)S(1)}, bf16[256,6,1024]{2,0,1:T(8,128)(2,1)}, u32[]{:S(2)}) copy-start(bf16[256,6,1024]{2,0,1:T(8,128)(2,1)} %param.4) | copy-start | bytes 9437188
  109.0 1.1 copy-start.3
  113.6 81.0 %reduce-scatter.5.cloned.1.call-start = ((), (), s32[]{:S(2)}) async-start(), calls=%async_computation.6 | async-start | bytes 163840 | tf_op jit(solution)/shard_map/reduce_scatter | solution.py:46
Sparse Core Ops, SparseCore 0:
  24.2 43.8 all-gather.1
  113.7 60.0 reduce-scatter.2
  176.0 18.5 reduce-scatter.4
where the time goes:
time: 203 us
  waiting for transfers between devices  118 us (58%)
  local copies, waits for them, and re-layouts  30.5 us (15%)
  matrix products  25.4 us (13%)
  between operations  13.8 us (7%)
  starting transfers between devices  10.3 us (5%)
  other arithmetic  4.54 us (2%)
    reduce_scatter x1, waiting for transfers between devices, per_device(): lax.psum_scatter(param_part.astype(jnp.bfloat16), 'expert', scatter_dimen...  60.1 us
    all_gather x1, waiting for transfers between devices, per_device(): all_params = lax.all_gather(slot_params, 'expert', axis=0, tiled=True)  45.9 us
    unnamed x12, local copies, waits for them, and re-layouts  20.2 us
    dot_general x1, matrix products, per_device(): jnp.einsum('tbs,tbd->sbd', combine_low, grad_out, preferred_element_type=...  11.4 us
    reshape x1, local copies, waits for them, and re-layouts, return_grads(): shaped = grad_slot.reshape(owners, all_slots // owners, img_rows, width)  6.69 us
    reduce_scatter x1, waiting for transfers between devices, per_device(): lax.psum_scatter(owned, 'dp', scatter_dimension=1, tiled=True)  6.62 us
    all_to_all x1, starting transfers between devices, fetch_outputs(): lax.all_to_all(shaped, 'expert', split_axis=1, concat_axis=0, tiled=True)  5.2 us
    dot_general x1, matrix products, per_device(): jnp.einsum('tbs,sd->tbd', grad_logits, all_params, preferred_element_type...  5.17 us
  transfers between devices with their start and end apart: 5, of which 4 were waited for; matrix products, arithmetic and copies ran while one was open for 24% of the time, Pallas kernels for 0%

commit v1 on v0

v1 whole, which is shorter than its diff:
```python
import functools

import jax
import jax.numpy as jnp
from jax import lax
from jax.experimental import pallas as pl
from jax.experimental.pallas import tpu as pltpu
from jax.sharding import PartitionSpec as P

BF = jnp.bfloat16
F32 = jnp.float32
GROUP = 16


def flip(index, mask, size):
    total, bit = 0, 1
    while bit < size:
        total = total + ((index // bit + mask // bit) % 2) * bit
        bit *= 2
    return total


def send_order(n, core):
    if n != 8:
        return list(range(n - 1, 0, -1))
    masks = []
    for low in range(2):
        masks += [6 + low - 4 * core, 2 + low + 2 * core, 4 + low + 2 * core]
    return masks + [1]


def rows_last(lhs, rhs):
    return lax.dot_general(lhs, rhs, (((1,), (1,)), ((), ())), preferred_element_type=F32)


def exchange_kernel(
    n, m, tok_hbm, go_hbm, so_hbm, par_hbm,
    grec, gt_out, gp_out,
    tok, go, so, par, allp, stage, rows, gs, comb, gt, acc, psend, precv, xsend, xrecv, gp,
    local_sem, p_send, p_recv, q_send, q_recv, a_send, a_recv, g_send, g_recv,
    z_send, z_recv, x_send, x_recv,
):
    me = lax.axis_index("expert")
    mz = lax.axis_index("dp")
    core = me % 2
    imgs = tok.shape[0]
    own = par.shape[0]
    all_img = so.shape[1]
    cols = allp.shape[1] // m
    width = allp.shape[1]
    slots = allp.shape[0]
    my_cols = pl.ds(pl.multiple_of(mz * cols, 128), cols)
    my_rows = pl.ds(pl.multiple_of(me * own, GROUP), own)

    loads = [
        pltpu.make_async_copy(src, dst, local_sem.at[i])
        for i, (src, dst) in enumerate([(par_hbm, par), (so_hbm, so), (tok_hbm, tok), (go_hbm, go)])
    ]
    for load in loads:
        load.start()

    barrier = pltpu.get_barrier_semaphore()
    for k in range(1, n):
        pl.semaphore_signal(barrier, inc=1, device_id=(mz, flip(me, k, n)), device_id_type=pl.DeviceIdType.MESH)
    for k in range(1, m):
        pl.semaphore_signal(barrier, inc=1, device_id=(flip(mz, k, m), me), device_id_type=pl.DeviceIdType.MESH)
    pl.semaphore_wait(barrier, n + m - 2)

    def to_expert(src, dst, send, recv, k):
        return pltpu.make_async_remote_copy(
            src_ref=src, dst_ref=dst, send_sem=send.at[k], recv_sem=recv.at[k],
            device_id=(mz, flip(me, k, n)), device_id_type=pl.DeviceIdType.MESH,
        )

    def to_dp(src, dst, send, recv, k):
        return pltpu.make_async_remote_copy(
            src_ref=src, dst_ref=dst, send_sem=send.at[k], recv_sem=recv.at[k],
            device_id=(flip(mz, k, m), me), device_id_type=pl.DeviceIdType.MESH,
        )

    loads[0].wait()
    p_copies = [to_expert(par.at[:, my_cols], allp.at[my_rows, my_cols], p_send, p_recv, k) for k in range(1, n)]
    for copy in p_copies:
        copy.start()
    allp[my_rows, my_cols] = par[:, my_cols]

    loads[1].wait()
    out_r = lax.broadcasted_iota(jnp.int32, (imgs * GROUP, GROUP * all_img), 0)
    in_c = lax.broadcasted_iota(jnp.int32, (imgs * GROUP, GROUP * all_img), 1)
    base = in_c - (out_r % GROUP) * all_img - out_r // GROUP

    def relayout(dest, out):
        pick = jnp.where(base == dest * imgs, 1.0, 0.0).astype(BF)

        def one(g, carry):
            s0 = pl.multiple_of(g * GROUP, GROUP)
            block = so[pl.ds(s0, GROUP)].reshape(GROUP * all_img, width)
            moved = jnp.dot(pick, block, preferred_element_type=F32).astype(BF)
            out[:, pl.ds(s0, GROUP), :] = moved.reshape(imgs, GROUP, width)
            return carry

        lax.fori_loop(0, own // GROUP, one, 0)

    order = send_order(n, core)
    a_copies = []
    for k in order:
        relayout(flip(me, k, n), stage.at[k])
        copy = to_expert(stage.at[k], rows.at[me], a_send, a_recv, k)
        copy.start()
        a_copies.append(copy)
    relayout(me, rows.at[me])

    for copy in p_copies:
        copy.wait_recv()
    q_copies = [to_dp(allp.at[:, my_cols], allp.at[:, my_cols], q_send, q_recv, k) for k in range(1, m)]
    for copy in q_copies:
        copy.start()
    loads[2].wait()
    loads[3].wait()
    for copy in q_copies:
        copy.wait_recv()

    def forward(b, carry):
        logits = rows_last(allp[...], tok[b])
        peak = jnp.max(logits, axis=0, keepdims=True)
        raised = jnp.exp(logits - peak)
        weights = raised / jnp.sum(raised, axis=0, keepdims=True)
        comb[b] = weights
        grads = jnp.dot(weights.astype(BF), go[b], preferred_element_type=F32).astype(BF)
        gs[:, b] = grads.reshape(n, own, width)
        return carry

    lax.fori_loop(0, imgs, forward, 0)

    keep = pltpu.make_async_copy(gs.at[me], grec.at[me], local_sem.at[4])
    keep.start()
    g_copies = []
    for k in order:
        copy = to_expert(gs.at[flip(me, k, n)], grec.at[me], g_send, g_recv, k)
        copy.start()
        g_copies.append(copy)

    for copy in a_copies:
        copy.wait_recv()
    acc[...] = jnp.zeros_like(acc)

    def backward(b, carry):
        grad_comb = rows_last(rows[:, b].reshape(slots, width), go[b])
        weights = comb[b]
        rowdot = jnp.sum(weights * grad_comb, axis=0, keepdims=True)
        wide = weights * (grad_comb - rowdot)
        acc[...] += jnp.dot(wide.astype(BF), tok[b], preferred_element_type=F32)
        gt[b] = jnp.dot(wide.T.astype(BF), allp[...], preferred_element_type=F32).astype(BF)
        return carry

    lax.fori_loop(0, imgs, backward, 0)

    for k in range(1, m):
        there = flip(mz, k, m)
        psend[k] = acc[:, pl.ds(pl.multiple_of(there * cols, 128), cols)].astype(BF)
    z_copies = [to_dp(psend.at[k], precv.at[k], z_send, z_recv, k) for k in range(1, m)]
    for copy in z_copies:
        copy.start()
    put = pltpu.make_async_copy(gt, gt_out, local_sem.at[5])
    put.start()
    for copy in z_copies:
        copy.wait_recv()
    total = acc[:, my_cols]
    for k in range(1, m):
        total = total + precv[k].astype(F32)
    acc[:, my_cols] = total
    for k in range(1, n):
        there = flip(me, k, n)
        xsend[k] = acc[pl.ds(pl.multiple_of(there * own, GROUP), own), my_cols].astype(BF)
    x_copies = [to_expert(xsend.at[k], xrecv.at[k], x_send, x_recv, k) for k in range(1, n)]
    for copy in x_copies:
        copy.start()
    for copy in x_copies:
        copy.wait_recv()
    owned = acc[my_rows, my_cols]
    for k in range(1, n):
        owned = owned + xrecv[k].astype(F32)
    gp[...] = owned
    give = pltpu.make_async_copy(gp, gp_out, local_sem.at[6])
    give.start()

    for copy in g_copies:
        copy.wait_recv()
    for copy in p_copies + a_copies + q_copies + g_copies + z_copies + x_copies:
        copy.wait_send()
    keep.wait()
    put.wait()
    give.wait()


def exchange(n, m, tok, go, so, par):
    imgs, patches, width = tok.shape
    own, all_img, _ = so.shape
    slots, cols = own * n, width // m
    dma = pltpu.SemaphoreType.DMA
    return pl.pallas_call(
        functools.partial(exchange_kernel, n, m),
        out_shape=(
            jax.ShapeDtypeStruct((n, imgs, own, width), BF),
            jax.ShapeDtypeStruct((imgs, patches, width), BF),
            jax.ShapeDtypeStruct((own, cols), F32),
        ),
        in_specs=[pl.BlockSpec(memory_space=pl.ANY)] * 4,
        out_specs=(pl.BlockSpec(memory_space=pl.ANY),) * 3,
        scratch_shapes=[
            pltpu.VMEM((imgs, patches, width), BF),
            pltpu.VMEM((imgs, patches, width), BF),
            pltpu.VMEM((own, all_img, width), BF),
            pltpu.VMEM((own, width), BF),
            pltpu.VMEM((slots, width), BF),
            pltpu.VMEM((n, imgs, own, width), BF),
            pltpu.VMEM((n, imgs, own, width), BF),
            pltpu.VMEM((n, imgs, own, width), BF),
            pltpu.VMEM((imgs, slots, patches), F32),
            pltpu.VMEM((imgs, patches, width), BF),
            pltpu.VMEM((slots, width), F32),
            pltpu.VMEM((m, slots, cols), BF),
            pltpu.VMEM((m, slots, cols), BF),
            pltpu.VMEM((n, own, cols), BF),
            pltpu.VMEM((n, own, cols), BF),
            pltpu.VMEM((own, cols), F32),
            dma((7,)),
            dma((n,)), dma((n,)), dma((m,)), dma((m,)),
            dma((n,)), dma((n,)), dma((n,)), dma((n,)),
            dma((m,)), dma((m,)), dma((n,)), dma((n,)),
        ],
        compiler_params=pltpu.CompilerParams(
            collective_id=0, has_side_effects=True, vmem_limit_bytes=66 * 1000 * 1000
        ),
    )(tok, go, so, par)


def settle_kernel(arrived, gp_in, out, gp_out):
    all_img, group, width = arrived.shape
    span = GROUP * group
    row = lax.broadcasted_iota(jnp.int32, (span, span), 0)
    col = lax.broadcasted_iota(jnp.int32, (span, span), 1)
    pick = jnp.where(col == (row % GROUP) * group + row // GROUP, 1.0, 0.0).astype(BF)
    for at in range(0, all_img, GROUP):
        block = arrived[at : at + GROUP].reshape(span, width)
        moved = jnp.dot(pick, block, preferred_element_type=F32).astype(BF)
        out[:, at : at + GROUP, :] = moved.reshape(group, GROUP, width)
    gp_out[...] = gp_in[...]


def settle(arrived, grad_par):
    all_img, own, width = arrived.shape
    small = pl.BlockSpec((GROUP, grad_par.shape[1]), lambda i: (i, 0))
    return pl.pallas_call(
        settle_kernel,
        grid=(own // GROUP,),
        out_shape=(
            jax.ShapeDtypeStruct((own, all_img, width), BF),
            jax.ShapeDtypeStruct(grad_par.shape, F32),
        ),
        in_specs=[pl.BlockSpec((all_img, GROUP, width), lambda i: (0, i, 0)), small],
        out_specs=(pl.BlockSpec((GROUP, all_img, width), lambda i: (i, 0, 0)), small),
    )(arrived, grad_par)


def per_device(n, m, tokens, grad_out, slot_out, slot_params):
    tok = jnp.transpose(tokens, (1, 0, 2))
    go = jnp.transpose(grad_out, (1, 0, 2))
    arrived, grad_tok, grad_par = exchange(n, m, tok, go, slot_out, slot_params)
    own, all_img, width = slot_out.shape
    grad_slot, grad_par = settle(arrived.reshape(all_img, own, width), grad_par)
    return jnp.transpose(grad_tok, (1, 0, 2)), grad_slot, grad_par


def solution(mesh):
    return jax.shard_map(
        functools.partial(per_device, mesh.shape["expert"], mesh.shape["dp"]),
        mesh=mesh,
        in_specs=(
            P(None, ("dp", "expert"), None),
            P(None, ("dp", "expert"), None),
            P("expert", "dp", None),
            P("expert", None),
        ),
        out_specs=(P(None, ("dp", "expert"), None), P("expert", "dp", None), P("expert", "dp")),
        check_vma=False,
    )
```

time: 203 us -> 159 us (0.78)
  Pallas kernels: 0 us -> 157 us
  waiting for transfers between devices: 118 us -> 0 us
  local copies, waits for them, and re-layouts: 30.5 us -> 1.67 us
  matrix products: 25.4 us -> 0 us
  between operations: 13.8 us -> 0.65 us
  starting transfers between devices: 10.3 us -> 0 us
  other arithmetic: 4.54 us -> 0 us
    pallas_call x0 -> x2, Pallas kernels: none -> 157 us  [the longest x1 150 us: exchange(): pl.pallas_call(functools.partial(exchange_kernel, n, m), out_shape=(jax.S...]
    reduce_scatter x2 -> x0, waiting for transfers between devices: 66.8 us -> none  [the longest x1 60.1 us: per_device(): lax.psum_scatter(param_part.astype(jnp.bfloat16), 'expert', scatter_dimen...]
    all_gather x1 -> x0, waiting for transfers between devices: 45.9 us -> none  [per_device(): all_params = lax.all_gather(slot_params, 'expert', axis=0, tiled=True)]
    dot_general x5 -> x0, matrix products: 25.4 us -> none  [the longest x1 11.4 us: per_device(): jnp.einsum('tbs,tbd->sbd', combine_low, grad_out, preferred_element_type=...]
    unnamed x12 -> x3, local copies, waits for them, and re-layouts: 20.2 us -> 1.67 us
    all_to_all x2 -> x0, starting transfers between devices: 9.99 us -> none  [the longest x1 5.2 us: fetch_outputs(): lax.all_to_all(shaped, 'expert', split_axis=1, concat_axis=0, tiled=True)]
    reshape x1 -> x0, local copies, waits for them, and re-layouts: 6.69 us -> none  [return_grads(): shaped = grad_slot.reshape(owners, all_slots // owners, img_rows, width)]
    all_to_all x2 -> x0, waiting for transfers between devices: 4.6 us -> none  [the longest x1 4.6 us: fetch_outputs(): lax.all_to_all(shaped, 'expert', split_axis=1, concat_axis=0, tiled=True)]
  transfers between devices with their start and end apart: 5 -> 0, of which waited for: 4 -> 0; matrix products, arithmetic and copies ran while one was open for 24% -> 0% of each run, Pallas kernels for 0% -> 0%
where the time goes in v1:
time: 159 us
  Pallas kernels  157 us (99%)
  local copies, waits for them, and re-layouts  1.67 us (1%)
    pallas_call x1, Pallas kernels, exchange(): pl.pallas_call(functools.partial(exchange_kernel, n, m), out_shape=(jax.S...  150 us
    pallas_call x1, Pallas kernels, settle(): pl.pallas_call(settle_kernel, grid=(own // GROUP,), out_shape=(jax.ShapeD...  7.05 us

profile of v1, /device:TPU:0, one launch (start us, length us, event | category | flops | bytes accessed | tf_op | source)
XLA Modules:
  0.0 159.1 jit_solution(1551563639141002270)
XLA Ops:
  0.6 149.8 %shard_map.67 = (bf16[8,6,64,1024]{3,2,1,0:T(8,128)(2,1)}, bf16[6,256,1024]{2,1,0:T(8,128)(2,1)}, f32[64,256]{1,0:T(8,128)}) custom-call(bf16[6,256,1024]{2,1,0:T(8,128)(2,1)} %bitcast.6, bf16[6,256,1024]{2,1,0:T(8,128)(2,1)} %bitcast.7, bf16[64,48,1024]{2,1,0:T(8,128)(2,1)} %so_hbm.1, bf16[64,1024]{1,0:T(8,128)(2,1)} %par_hbm.1), custom_call_target="tpu_custom_call" | custom-call | tf_op jit(solution)/shard_map/pallas_call | solution.py:201
  150.4 0.0 copy-start
  150.4 7.1 %shard_map.68 = (bf16[64,48,1024]{2,1,0:T(8,128)(2,1)}, f32[64,256]{1,0:T(8,128)}) custom-call(bf16[48,64,1024]{2,1,0:T(8,128)(2,1)} %bitcast.4, f32[64,256]{1,0:T(8,128)} %get-tuple-element.10.gp_in), custom_call_target="tpu_custom_call" | custom-call | tf_op jit(solution)/shard_map/pallas_call | solution.py:254
  157.5 0.0 copy-done
  157.5 1.7 %copy.8 = bf16[256,6,1024]{2,0,1:T(8,128)(2,1)} copy(bf16[256,6,1024]{2,0,1:T(8,128)(2,1)S(1)} %bitcast.5) | data formatting | bytes 6291456
Async XLA Ops:
  150.4 7.1 %copy-start = (bf16[6,256,1024]{2,1,0:T(8,128)(2,1)S(1)}, bf16[6,256,1024]{2,1,0:T(8,128)(2,1)}, u32[]{:S(2)}) copy-start(bf16[6,256,1024]{2,1,0:T(8,128)(2,1)} %get-tuple-element.8) | copy-start | bytes 9437188

commit v2 on v1

--- a/solution.py
+++ b/solution.py
@@ -235,6 +235,324 @@
     )(tok, go, so, par)
 
 
+AXES = ((2, (4, 5, 1)), (4, (2, 3, 1)))
+
+
+def side_spot(which, index):
+    high = index // 4 if which == 0 else (index // 2) % 2
+    return high * 2 + index % 2
+
+
+def paired_kernel(
+    n, m, tok_hbm, go_hbm, so_hbm, par_hbm,
+    grec, gt_out, gp_out,
+    tok, go, mate, so, par, allp, stage, rows, gs, comb, gcf, low, low_send, gc_send, gc_recv,
+    gt, acc, psend, precv, xsend, xrecv, gp,
+    local_sem, keep_sem, p_send, p_recv, q_send, q_recv, o_send, o_recv, a_send, a_recv, w_send, w_recv,
+    c_send, c_recv, g_send, g_recv, z_send, z_recv, x_send, x_recv,
+):
+    me = lax.axis_index("expert")
+    mz = lax.axis_index("dp")
+    imgs = tok.shape[0]
+    half = imgs // 2
+    own = par.shape[0]
+    all_img = so.shape[1]
+    slots, width = allp.shape
+    patches = tok.shape[1]
+    cols = width // m
+    quarter = slots // 4
+    my_cols = pl.ds(pl.multiple_of(mz * cols, 128), cols)
+    my_rows = pl.ds(pl.multiple_of(me * own, GROUP), own)
+    sides = ((me // 2) % 2, me // 4)
+
+    def piece(which, other, p):
+        side = 1 - sides[which] if other else sides[which]
+        start = p * 2 * quarter + side * quarter if which == 0 else side * 2 * quarter + p * quarter
+        return pl.ds(pl.multiple_of(start, quarter), quarter)
+
+    loads = [
+        pltpu.make_async_copy(src, dst, local_sem.at[i])
+        for i, (src, dst) in enumerate([(par_hbm, par), (so_hbm, so), (tok_hbm, tok), (go_hbm, go)])
+    ]
+    for i in (0, 3, 1, 2):
+        loads[i].start()
+
+    barrier = pltpu.get_barrier_semaphore()
+    for k in range(1, n):
+        pl.semaphore_signal(barrier, inc=1, device_id=(mz, flip(me, k, n)), device_id_type=pl.DeviceIdType.MESH)
+    for k in range(1, m):
+        pl.semaphore_signal(barrier, inc=1, device_id=(flip(mz, k, m), me), device_id_type=pl.DeviceIdType.MESH)
+    pl.semaphore_wait(barrier, n + m - 2)
+
+    def to_expert(src, dst, send, recv, k):
+        return pltpu.make_async_remote_copy(
+            src_ref=src, dst_ref=dst, send_sem=send, recv_sem=recv,
+            device_id=(mz, flip(me, k, n)), device_id_type=pl.DeviceIdType.MESH,
+        )
+
+    def to_dp(src, dst, send, recv):
+        return [
+            pltpu.make_async_remote_copy(
+                src_ref=src(k), dst_ref=dst(k), send_sem=send.at[k], recv_sem=recv.at[k],
+                device_id=(flip(mz, k, m), me), device_id_type=pl.DeviceIdType.MESH,
+            )
+            for k in range(1, m)
+        ]
+
+    sent = []
+
+    def launch(copies):
+        for copy in copies:
+            copy.start()
+        sent.extend(copies)
+        return copies
+
+    def arrive(copies):
+        for copy in copies:
+            copy.wait_recv()
+
+    loads[0].wait()
+    p_copies = launch([
+        to_expert(par.at[:, my_cols], allp.at[my_rows, my_cols], p_send.at[k], p_recv.at[k], k) for k in range(1, n)
+    ])
+    allp[my_rows, my_cols] = par[:, my_cols]
+    loads[3].wait()
+    o_copies = launch([
+        to_expert(go.at[pl.ds(q * half, half)], mate.at[q], o_send.at[q], o_recv.at[q], AXES[q][0]) for q in range(2)
+    ])
+
+    loads[1].wait()
+    out_r = lax.broadcasted_iota(jnp.int32, (imgs * GROUP, GROUP * all_img), 0)
+    in_c = lax.broadcasted_iota(jnp.int32, (imgs * GROUP, GROUP * all_img), 1)
+    base = in_c - (out_r % GROUP) * all_img - (out_r // GROUP) % half
+    first = out_r < half * GROUP
+
+    def relayout(q, dest, out):
+        own_at = dest * imgs + q * half
+        mate_at = flip(dest, AXES[q][0], n) * imgs + q * half
+        pick = jnp.where(base == jnp.where(first, own_at, mate_at), 1.0, 0.0).astype(BF)
+
+        def one(g, carry):
+            s0 = pl.multiple_of(g * GROUP, GROUP)
+            block = so[pl.ds(s0, GROUP)].reshape(GROUP * all_img, width)
+            moved = jnp.dot(pick, block, preferred_element_type=F32).astype(BF)
+            out[:, pl.ds(s0, GROUP), :] = moved.reshape(imgs, GROUP, width)
+            return carry
+
+        lax.fori_loop(0, own // GROUP, one, 0)
+
+    a_copies = []
+    for i in range(3):
+        for q in range(2):
+            k = AXES[q][1][i]
+            relayout(q, flip(me, k, n), stage.at[q, i])
+            a_copies += launch([
+                to_expert(stage.at[q, i], rows.at[q, side_spot(q, me)], a_send.at[q, i], a_recv.at[q, i], k)
+            ])
+    for q in range(2):
+        relayout(q, me, rows.at[q, side_spot(q, me)])
+
+    arrive(p_copies)
+    q_copies = launch(to_dp(lambda k: allp.at[:, my_cols], lambda k: allp.at[:, my_cols], q_send, q_recv))
+    loads[2].wait()
+    arrive(q_copies)
+
+    w_copies = []
+    for q in range(2):
+
+        def forward(t, carry):
+            b = q * half + t
+            logits = rows_last(allp[...], tok[b])
+            peak = jnp.max(logits, axis=0, keepdims=True)
+            raised = jnp.exp(logits - peak)
+            comb[b] = raised / jnp.sum(raised, axis=0, keepdims=True)
+            for p in range(2):
+                low[q, t, p * quarter : (p + 1) * quarter] = comb[b, piece(q, False, p)].astype(BF)
+                low_send[q, t, p * quarter : (p + 1) * quarter] = comb[b, piece(q, True, p)].astype(BF)
+            return carry
+
+        lax.fori_loop(0, half, forward, 0)
+        w_copies += launch([
+            to_expert(low_send.at[q], low.at[q, pl.ds(half, half)], w_send.at[q], w_recv.at[q], AXES[q][0])
+        ])
+
+    def slot_grads(q, i, grads_in):
+        out = jnp.dot(low[q, i], grads_in, preferred_element_type=F32).astype(BF)
+        gs[q, :, i] = out.reshape(4, own, width)
+
+    def comb_grads(q, i, grads_in):
+        return rows_last(rows[q, :, i].reshape(4 * own, width), grads_in)
+
+    for q in range(2):
+
+        def own_slots(t, carry):
+            slot_grads(q, t, go[q * half + t])
+            return carry
+
+        lax.fori_loop(0, half, own_slots, 0)
+
+    arrive(o_copies)
+    arrive(a_copies)
+    c_copies = []
+    for q in range(2):
+
+        def mate_comb(t, carry):
+            gc_send[q, t] = comb_grads(q, half + t, mate[q, t]).astype(BF)
+            return carry
+
+        lax.fori_loop(0, half, mate_comb, 0)
+        c_copies += launch([to_expert(gc_send.at[q], gc_recv.at[q], c_send.at[q], c_recv.at[q], AXES[q][0])])
+
+    keeps = []
+
+    def return_grads(h):
+        copies = []
+        for i in range(3):
+            for q in range(2):
+                k = AXES[q][1][i]
+                holder = flip(me, AXES[q][0], n) if h else me
+                part, images = pl.ds(h * half, half), pl.ds(q * half, half)
+                copies += launch([
+                    to_expert(
+                        gs.at[q, side_spot(q, flip(me, k, n)), part], grec.at[holder, images],
+                        g_send.at[h, q, i], g_recv.at[h, q, i], k,
+                    )
+                ])
+        for q in range(2):
+            holder = flip(me, AXES[q][0], n) if h else me
+            keep = pltpu.make_async_copy(
+                gs.at[q, side_spot(q, me), pl.ds(h * half, half)],
+                grec.at[holder, pl.ds(q * half, half)], keep_sem.at[h, q],
+            )
+            keep.start()
+            keeps.append(keep)
+        return copies
+
+    g_copies = return_grads(0)
+    arrive(w_copies)
+    for q in range(2):
+
+        def mate_slots(t, carry):
+            slot_grads(q, half + t, mate[q, t])
+            return carry
+
+        lax.fori_loop(0, half, mate_slots, 0)
+    g_copies += return_grads(1)
+
+    for q in range(2):
+
+        def own_comb(t, carry):
+            grads = comb_grads(q, t, go[q * half + t])
+            for p in range(2):
+                gcf[q * half + t, piece(q, False, p)] = grads[p * quarter : (p + 1) * quarter]
+            return carry
+
+        lax.fori_loop(0, half, own_comb, 0)
+    acc[...] = jnp.zeros_like(acc)
+    arrive(c_copies)
+    for q in range(2):
+
+        def backward(t, carry):
+            b = q * half + t
+            for p in range(2):
+                gcf[b, piece(q, True, p)] = gc_recv[q, t, p * quarter : (p + 1) * quarter].astype(F32)
+            grad_comb = gcf[b]
+            weights = comb[b]
+            rowdot = jnp.sum(weights * grad_comb, axis=0, keepdims=True)
+            wide = weights * (grad_comb - rowdot)
+            gcf[b] = wide
+            acc[...] += jnp.dot(wide.astype(BF), tok[b], preferred_element_type=F32)
+            return carry
+
+        lax.fori_loop(0, half, backward, 0)
+
+    for k in range(1, m):
+        there = flip(mz, k, m)
+        psend[k] = acc[:, pl.ds(pl.multiple_of(there * cols, 128), cols)].astype(BF)
+    z_copies = launch(to_dp(lambda k: psend.at[k], lambda k: precv.at[k], z_send, z_recv))
+
+    def token_grads(b, carry):
+        gt[b] = jnp.dot(gcf[b].T.astype(BF), allp[...], preferred_element_type=F32).astype(BF)
+        return carry
+
+    lax.fori_loop(0, imgs, token_grads, 0)
+    put = pltpu.make_async_copy(gt, gt_out, local_sem.at[5])
+    put.start()
+    arrive(z_copies)
+    total = acc[:, my_cols]
+    for k in range(1, m):
+        total = total + precv[k].astype(F32)
+    acc[:, my_cols] = total
+    for k in range(1, n):
+        there = flip(me, k, n)
+        xsend[k] = acc[pl.ds(pl.multiple_of(there * own, GROUP), own), my_cols].astype(BF)
+    x_copies = launch([to_expert(xsend.at[k], xrecv.at[k], x_send.at[k], x_recv.at[k], k) for k in range(1, n)])
+    arrive(x_copies)
+    owned = acc[my_rows, my_cols]
+    for k in range(1, n):
+        owned = owned + xrecv[k].astype(F32)
+    gp[...] = owned
+    give = pltpu.make_async_copy(gp, gp_out, local_sem.at[6])
+    give.start()
+
+    arrive(g_copies)
+    for copy in sent:
+        copy.wait_send()
+    for keep in keeps:
+        keep.wait()
+    put.wait()
+    give.wait()
+
+
+def paired_exchange(n, m, tok, go, so, par):
+    imgs, patches, width = tok.shape
+    own, all_img, _ = so.shape
+    slots, cols, half = own * n, width // m, imgs // 2
+    dma = pltpu.SemaphoreType.DMA
+    return pl.pallas_call(
+        functools.partial(paired_kernel, n, m),
+        out_shape=(
+            jax.ShapeDtypeStruct((n, imgs, own, width), BF),
+            jax.ShapeDtypeStruct((imgs, patches, width), BF),
+            jax.ShapeDtypeStruct((own, cols), F32),
+        ),
+        in_specs=[pl.BlockSpec(memory_space=pl.ANY)] * 4,
+        out_specs=(pl.BlockSpec(memory_space=pl.ANY),) * 3,
+        scratch_shapes=[
+            pltpu.VMEM((imgs, patches, width), BF),
+            pltpu.VMEM((imgs, patches, width), BF),
+            pltpu.VMEM((2, half, patches, width), BF),
+            pltpu.VMEM((own, all_img, width), BF),
+            pltpu.VMEM((own, width), BF),
+            pltpu.VMEM((slots, width), BF),
+            pltpu.VMEM((2, 3, imgs, own, width), BF),
+            pltpu.VMEM((2, 4, imgs, own, width), BF),
+            pltpu.VMEM((2, 4, imgs, own, width), BF),
+            pltpu.VMEM((imgs, slots, patches), F32),
+            pltpu.VMEM((imgs, slots, patches), F32),
+            pltpu.VMEM((2, imgs, slots // 2, patches), BF),
+            pltpu.VMEM((2, half, slots // 2, patches), BF),
+            pltpu.VMEM((2, half, slots // 2, patches), BF),
+            pltpu.VMEM((2, half, slots // 2, patches), BF),
+            pltpu.VMEM((imgs, patches, width), BF),
+            pltpu.VMEM((slots, width), F32),
+            pltpu.VMEM((m, slots, cols), BF),
+            pltpu.VMEM((m, slots, cols), BF),
+            pltpu.VMEM((n, own, cols), BF),
+            pltpu.VMEM((n, own, cols), BF),
+            pltpu.VMEM((own, cols), F32),
+            dma((7,)), dma((2, 2)),
+            dma((n,)), dma((n,)), dma((m,)), dma((m,)),
+            dma((2,)), dma((2,)), dma((2, 3)), dma((2, 3)), dma((2,)), dma((2,)),
+            dma((2,)), dma((2,)), dma((2, 2, 3)), dma((2, 2, 3)),
+            dma((m,)), dma((m,)), dma((n,)), dma((n,)),
+        ],
+        compiler_params=pltpu.CompilerParams(
+            collective_id=0, has_side_effects=True, vmem_limit_bytes=66 * 1000 * 1000
+        ),
+    )(tok, go, so, par)
+
+
 def settle_kernel(arrived, gp_in, out, gp_out):
     all_img, group, width = arrived.shape
     span = GROUP * group
@@ -266,7 +584,8 @@
 def per_device(n, m, tokens, grad_out, slot_out, slot_params):
     tok = jnp.transpose(tokens, (1, 0, 2))
     go = jnp.transpose(grad_out, (1, 0, 2))
-    arrived, grad_tok, grad_par = exchange(n, m, tok, go, slot_out, slot_params)
+    plan = paired_exchange if n == 8 and tok.shape[0] % 2 == 0 else exchange
+    arrived, grad_tok, grad_par = plan(n, m, tok, go, slot_out, slot_params)
     own, all_img, width = slot_out.shape
     grad_slot, grad_par = settle(arrived.reshape(all_img, own, width), grad_par)
     return jnp.transpose(grad_tok, (1, 0, 2)), grad_slot, grad_par

time: 159 us -> 142 us (0.89)
  Pallas kernels: 157 us -> 140 us
    pallas_call x1, Pallas kernels: 150 us -> 133 us  [paired_exchange(): pl.pallas_call(functools.partial(paired_kernel, n, m), out_shape=(jax.Sha...]
where the time goes in v2:
time: 142 us
  Pallas kernels  140 us (99%)
  local copies, waits for them, and re-layouts  1.67 us (1%)
    pallas_call x1, Pallas kernels, paired_exchange(): pl.pallas_call(functools.partial(paired_kernel, n, m), out_shape=(jax.Sha...  133 us
    pallas_call x1, Pallas kernels, settle(): pl.pallas_call(settle_kernel, grid=(own // GROUP,), out_shape=(jax.ShapeD...  7.05 us

profile of v2, /device:TPU:0, one launch (start us, length us, event | category | flops | bytes accessed | tf_op | source)
XLA Modules:
  0.0 142.3 jit_solution(14249572049629479077)
XLA Ops:
  0.6 132.9 %shard_map.67 = (bf16[8,6,64,1024]{3,2,1,0:T(8,128)(2,1)}, bf16[6,256,1024]{2,1,0:T(8,128)(2,1)}, f32[64,256]{1,0:T(8,128)}) custom-call(bf16[6,256,1024]{2,1,0:T(8,128)(2,1)} %bitcast.6, bf16[6,256,1024]{2,1,0:T(8,128)(2,1)} %bitcast.7, bf16[64,48,1024]{2,1,0:T(8,128)(2,1)} %so_hbm.1, bf16[64,1024]{1,0:T(8,128)(2,1)} %par_hbm.1), custom_call_target="tpu_custom_call" | custom-call | tf_op jit(solution)/shard_map/pallas_call | solution.py:512
  133.6 0.0 copy-start
  133.6 7.1 %shard_map.68 = (bf16[64,48,1024]{2,1,0:T(8,128)(2,1)}, f32[64,256]{1,0:T(8,128)}) custom-call(bf16[48,64,1024]{2,1,0:T(8,128)(2,1)} %bitcast.4, f32[64,256]{1,0:T(8,128)} %get-tuple-element.10.gp_in), custom_call_target="tpu_custom_call" | custom-call | tf_op jit(solution)/shard_map/pallas_call | solution.py:572
  140.6 0.0 copy-done
  140.6 1.7 %copy.8 = bf16[256,6,1024]{2,0,1:T(8,128)(2,1)} copy(bf16[256,6,1024]{2,0,1:T(8,128)(2,1)S(1)} %bitcast.5) | data formatting | bytes 6291456
Async XLA Ops:
  133.6 7.1 %copy-start = (bf16[6,256,1024]{2,1,0:T(8,128)(2,1)S(1)}, bf16[6,256,1024]{2,1,0:T(8,128)(2,1)}, u32[]{:S(2)}) copy-start(bf16[6,256,1024]{2,1,0:T(8,128)(2,1)} %get-tuple-element.8) | copy-start | bytes 9437188

commit v3 on v2

--- a/solution.py
+++ b/solution.py
@@ -247,8 +247,8 @@
     n, m, tok_hbm, go_hbm, so_hbm, par_hbm,
     grec, gt_out, gp_out,
     tok, go, mate, so, par, allp, stage, rows, gs, comb, gcf, low, low_send, gc_send, gc_recv,
-    gt, acc, psend, precv, xsend, xrecv, gp,
-    local_sem, keep_sem, p_send, p_recv, q_send, q_recv, o_send, o_recv, a_send, a_recv, w_send, w_recv,
+    gt, acc, ksend, krecv, red, psend, precv, xsend, xrecv, gp,
+    local_sem, keep_sem, p_send, p_recv, q_send, q_recv, f_send, f_recv, k_send, k_recv, o_send, o_recv, a_send, a_recv, w_send, w_recv,
     c_send, c_recv, g_send, g_recv, z_send, z_recv, x_send, x_recv,
 ):
     me = lax.axis_index("expert")
@@ -313,7 +313,8 @@
 
     loads[0].wait()
     p_copies = launch([
-        to_expert(par.at[:, my_cols], allp.at[my_rows, my_cols], p_send.at[k], p_recv.at[k], k) for k in range(1, n)
+        to_expert(par.at[:, my_cols], allp.at[my_rows, my_cols], p_send.at[k], p_recv.at[k], k)
+        for k in range(2, n, 2)
     ])
     allp[my_rows, my_cols] = par[:, my_cols]
     loads[3].wait()
@@ -353,9 +354,17 @@
         relayout(q, me, rows.at[q, side_spot(q, me)])
 
     arrive(p_copies)
-    q_copies = launch(to_dp(lambda k: allp.at[:, my_cols], lambda k: allp.at[:, my_cols], q_send, q_recv))
+    q_copies = []
+    for i in range(n // 2):
+        block = allp.at[pl.ds(pl.multiple_of(flip(me, 2 * i, n) * own, GROUP), own), my_cols]
+        q_copies += launch(to_dp(lambda k: block, lambda k: block, q_send.at[i], q_recv.at[i]))
     loads[2].wait()
     arrive(q_copies)
+    f_copies = []
+    for i in range(n // 2):
+        block = allp.at[pl.ds(pl.multiple_of(flip(me, 2 * i, n) * own, GROUP), own)]
+        f_copies += launch([to_expert(block, block, f_send.at[i], f_recv.at[i], 1)])
+    arrive(f_copies)
 
     w_copies = []
     for q in range(2):
@@ -466,9 +475,16 @@
 
         lax.fori_loop(0, half, backward, 0)
 
+    core = me % 2
+    for i in range(n // 2):
+        ksend[i] = acc[pl.ds(pl.multiple_of((2 * i + 1 - core) * own, GROUP), own)].astype(BF)
+    k_copies = launch([to_expert(ksend, krecv, k_send.at[0], k_recv.at[0], 1)])
+    arrive(k_copies)
+    for i in range(n // 2):
+        red[i] = acc[pl.ds(pl.multiple_of((2 * i + core) * own, GROUP), own)] + krecv[i].astype(F32)
     for k in range(1, m):
         there = flip(mz, k, m)
-        psend[k] = acc[:, pl.ds(pl.multiple_of(there * cols, 128), cols)].astype(BF)
+        psend[k] = red[:, :, pl.ds(pl.multiple_of(there * cols, 128), cols)].astype(BF)
     z_copies = launch(to_dp(lambda k: psend.at[k], lambda k: precv.at[k], z_send, z_recv))
 
     def token_grads(b, carry):
@@ -479,18 +495,19 @@
     put = pltpu.make_async_copy(gt, gt_out, local_sem.at[5])
     put.start()
     arrive(z_copies)
-    total = acc[:, my_cols]
+    total = red[:, :, my_cols]
     for k in range(1, m):
         total = total + precv[k].astype(F32)
-    acc[:, my_cols] = total
-    for k in range(1, n):
-        there = flip(me, k, n)
-        xsend[k] = acc[pl.ds(pl.multiple_of(there * own, GROUP), own), my_cols].astype(BF)
-    x_copies = launch([to_expert(xsend.at[k], xrecv.at[k], x_send.at[k], x_recv.at[k], k) for k in range(1, n)])
+    red[:, :, my_cols] = total
+    for k in range(2, n, 2):
+        xsend[k // 2] = red[flip(me, k, n) // 2, :, my_cols].astype(BF)
+    x_copies = launch([
+        to_expert(xsend.at[k // 2], xrecv.at[k // 2], x_send.at[k], x_recv.at[k], k) for k in range(2, n, 2)
+    ])
     arrive(x_copies)
-    owned = acc[my_rows, my_cols]
-    for k in range(1, n):
-        owned = owned + xrecv[k].astype(F32)
+    owned = red[me // 2, :, my_cols]
+    for k in range(2, n, 2):
+        owned = owned + xrecv[k // 2].astype(F32)
     gp[...] = owned
     give = pltpu.make_async_copy(gp, gp_out, local_sem.at[6])
     give.start()
@@ -536,13 +553,17 @@
             pltpu.VMEM((2, half, slots // 2, patches), BF),
             pltpu.VMEM((imgs, patches, width), BF),
             pltpu.VMEM((slots, width), F32),
-            pltpu.VMEM((m, slots, cols), BF),
-            pltpu.VMEM((m, slots, cols), BF),
-            pltpu.VMEM((n, own, cols), BF),
-            pltpu.VMEM((n, own, cols), BF),
+            pltpu.VMEM((n // 2, own, width), BF),
+            pltpu.VMEM((n // 2, own, width), BF),
+            pltpu.VMEM((n // 2, own, width), F32),
+            pltpu.VMEM((m, n // 2, own, cols), BF),
+            pltpu.VMEM((m, n // 2, own, cols), BF),
+            pltpu.VMEM((n // 2, own, cols), BF),
+            pltpu.VMEM((n // 2, own, cols), BF),
             pltpu.VMEM((own, cols), F32),
             dma((7,)), dma((2, 2)),
-            dma((n,)), dma((n,)), dma((m,)), dma((m,)),
+            dma((n,)), dma((n,)), dma((n // 2, m)), dma((n // 2, m)),
+            dma((n // 2,)), dma((n // 2,)), dma((1,)), dma((1,)),
             dma((2,)), dma((2,)), dma((2, 3)), dma((2, 3)), dma((2,)), dma((2,)),
             dma((2,)), dma((2,)), dma((2, 2, 3)), dma((2, 2, 3)),
             dma((m,)), dma((m,)), dma((n,)), dma((n,)),
@@ -554,15 +575,7 @@
 
 
 def settle_kernel(arrived, gp_in, out, gp_out):
-    all_img, group, width = arrived.shape
-    span = GROUP * group
-    row = lax.broadcasted_iota(jnp.int32, (span, span), 0)
-    col = lax.broadcasted_iota(jnp.int32, (span, span), 1)
-    pick = jnp.where(col == (row % GROUP) * group + row // GROUP, 1.0, 0.0).astype(BF)
-    for at in range(0, all_img, GROUP):
-        block = arrived[at : at + GROUP].reshape(span, width)
-        moved = jnp.dot(pick, block, preferred_element_type=F32).astype(BF)
-        out[:, at : at + GROUP, :] = moved.reshape(group, GROUP, width)
+    out[...] = jnp.swapaxes(arrived[...], 0, 1)
     gp_out[...] = gp_in[...]
 
 

time: 142 us -> 140 us (0.986)
  Pallas kernels: 140 us -> 137 us
    pallas_call x1, Pallas kernels: 133 us -> 131 us  [paired_exchange(): pl.pallas_call(functools.partial(paired_kernel, n, m), out_shape=(jax.Sha...]
where the time goes in v3:
time: 140 us
  Pallas kernels  137 us (98%)
  local copies, waits for them, and re-layouts  1.67 us (1%)
    pallas_call x1, Pallas kernels, paired_exchange(): pl.pallas_call(functools.partial(paired_kernel, n, m), out_shape=(jax.Sha...  131 us
    pallas_call x1, Pallas kernels, settle(): pl.pallas_call(settle_kernel, grid=(own // GROUP,), out_shape=(jax.ShapeD...  6.68 us

profile of v3, /device:TPU:0, one launch (start us, length us, event | category | flops | bytes accessed | tf_op | source)
XLA Modules:
  0.0 139.7 jit_solution(10817677100961227470)
XLA Ops:
  0.6 130.7 %shard_map.67 = (bf16[8,6,64,1024]{3,2,1,0:T(8,128)(2,1)}, bf16[6,256,1024]{2,1,0:T(8,128)(2,1)}, f32[64,256]{1,0:T(8,128)}) custom-call(bf16[6,256,1024]{2,1,0:T(8,128)(2,1)} %bitcast.6, bf16[6,256,1024]{2,1,0:T(8,128)(2,1)} %bitcast.7, bf16[64,48,1024]{2,1,0:T(8,128)(2,1)} %so_hbm.1, bf16[64,1024]{1,0:T(8,128)(2,1)} %par_hbm.1), custom_call_target="tpu_custom_call" | custom-call | tf_op jit(solution)/shard_map/pallas_call | solution.py:529
  131.4 0.0 copy-start
  131.4 6.7 %shard_map.68 = (bf16[64,48,1024]{2,1,0:T(8,128)(2,1)}, f32[64,256]{1,0:T(8,128)}) custom-call(bf16[48,64,1024]{2,1,0:T(8,128)(2,1)} %bitcast.4, f32[64,256]{1,0:T(8,128)} %get-tuple-element.10.gp_in), custom_call_target="tpu_custom_call" | custom-call | tf_op jit(solution)/shard_map/pallas_call | solution.py:585
  138.1 0.0 copy-done
  138.1 1.7 %copy.8 = bf16[256,6,1024]{2,0,1:T(8,128)(2,1)} copy(bf16[256,6,1024]{2,0,1:T(8,128)(2,1)S(1)} %bitcast.5) | data formatting | bytes 6291456
Async XLA Ops:
  131.4 6.7 %copy-start = (bf16[6,256,1024]{2,1,0:T(8,128)(2,1)S(1)}, bf16[6,256,1024]{2,1,0:T(8,128)(2,1)}, u32[]{:S(2)}) copy-start(bf16[6,256,1024]{2,1,0:T(8,128)(2,1)} %get-tuple-element.8) | copy-start | bytes 9437188
